TPU v7x, 32 devices: a whole 2x2x4 slice. The times are simulated.
32 devices in a mesh: row: 4 (over x, core), col: 8 (over z, y).
Axes of the slice: x: 2, y: 2, z: 4, core: 2. Of those that a mesh axis runs over, the one named last changes fastest.
Arguments:
- resistance: float32 [4096, 8192], P('row', 'col'), may hold values from 1 to 100
- source_mask: int32 [4096, 8192], P('row', 'col'), may hold values 0 or 1
- target_mask: int32 [4096, 8192], P('row', 'col'), may hold values 0 or 1
- centers: int32 [512, 2], P(('row', 'col')), may hold values from 0 to 8191, as said below
- live_counts: int32 [32], P(('row', 'col')), may hold values from 1 to 16, 128 in all
Outputs:
- current_map: float32 [4096, 8192], P('row', 'col')
Inputs may be any that keep to these rules, and one draw needn't show every extreme that they name: `centers`: the center of slot s lies inside the block of raster cells held by device s // 16 (numbered along row+col, row slowest). Slots 0 to live_counts[d] - 1 of device d are live; some device has all 16 slots live.
All inputs are finite; a program needn't handle non-finite values. No bound on the sum of `source_mask` or of `target_mask` on one device may be relied on, other than what follows from the above.
Results may differ from a plain program's by a relative error of at most 0.0003.
Values sent between devices are 32-bit elements; how exact they have to be, the bound alone decides.
A program may use at most 128 MiB of HBM per device.

v0:
```python
import functools

import jax
import jax.numpy as jnp
from jax import lax
from jax.experimental import pallas as pl
from jax.experimental.pallas import tpu as pltpu
from jax.sharding import PartitionSpec as P

RAD = 64
SIDE = 2 * RAD
ITERS = 24
LEAKAGE = 0.02
GROUP = 4
LANES = 128
TALL = SIDE + 8
WIDE = 2 * LANES
SHIFTS = ((0, -1), (0, 1), (-1, 0), (1, 0), (-1, -1), (-1, 1), (1, -1), (1, 1))


def roll(value, shift, axis):
    return pltpu.roll(value, shift % value.shape[axis], axis)


def lane_ids(shape):
    return lax.broadcasted_iota(jnp.int32, shape, 1)


def to_low(packed):
    return packed, roll(packed, RAD, 1)


def to_high(packed):
    return roll(packed, RAD, 1), packed


def pack_low(tile):
    half = tile.shape[0] // 2
    first, second = tile[:half], tile[half:]
    return jnp.where(lane_ids(first.shape) < RAD, first, roll(second, RAD, 1))


def pack_high(tile):
    half = tile.shape[0] // 2
    first, second = tile[:half], tile[half:]
    return jnp.where(lane_ids(first.shape) < RAD, roll(first, RAD, 1), second)


def neighbours():
    row, col = lax.axis_index("row"), lax.axis_index("col")
    rows, cols = lax.axis_size("row"), lax.axis_size("col")
    found = {}
    for (dr, dc) in SHIFTS:
        r, c = row + dr, col + dc
        found[(dr, dc)] = ((r >= 0) & (r < rows) & (c >= 0) & (c < cols), (r, c))
    return found


def greet(found):
    barrier = pltpu.get_barrier_semaphore()
    for at in SHIFTS:
        exists, device = found[at]

        @pl.when(exists)
        def _():
            pl.semaphore_signal(barrier, inc=1, device_id=device, device_id_type=pl.DeviceIdType.MESH)


def all_greeted(found):
    count = sum(found[at][0].astype(jnp.int32) for at in SHIFTS)
    pl.semaphore_wait(pltpu.get_barrier_semaphore(), count)


def transfers(found, pieces, halos, send_sems, recv_sems):
    made = []
    for k, at in enumerate(SHIFTS):
        exists, device = found[at]
        back = (-at[0], -at[1])
        made.append((exists, pltpu.make_async_remote_copy(
            src_ref=pieces[at],
            dst_ref=halos[back],
            send_sem=send_sems.at[k],
            recv_sem=recv_sems.at[SHIFTS.index(back)],
            device_id=device,
            device_id_type=pl.DeviceIdType.MESH,
        )))
    return made


def landings(found, pieces, halos, send_sems, recv_sems):
    made = []
    for k, at in enumerate(SHIFTS):
        exists, device = found[at]
        made.append((exists, pltpu.make_async_remote_copy(
            src_ref=pieces[at],
            dst_ref=halos[at],
            send_sem=send_sems.at[k],
            recv_sem=recv_sems.at[k],
            device_id=device,
            device_id_type=pl.DeviceIdType.MESH,
        )))
    return made


def start_all(copies):
    for exists, copy in copies:
        pl.when(exists)(copy.start)


def finish_all(copies, arrivals):
    for exists, copy in copies:
        pl.when(exists)(copy.wait_send)
    for exists, copy in arrivals:
        pl.when(exists)(copy.wait_recv)


def corner_of(centers, slot, rows, cols):
    return lax.rem(centers[slot, 0], rows) - RAD, lax.rem(centers[slot, 1], cols) - RAD


def is_inner(top, left, rows, cols):
    return (top >= 0) & (top <= rows - SIDE) & (left >= 0) & (left <= cols - SIDE)


def clamped(top, left, rows, cols):
    row = jnp.clip((top + RAD) // 8 * 8 - RAD, 0, rows - TALL)
    col = jnp.clip((left + LANES) // LANES * LANES - LANES, 0, cols - WIDE)
    return pl.multiple_of(row, 8), pl.multiple_of(col, LANES)


def total(values):
    return jnp.sum(jnp.sum(values, axis=0, keepdims=True), axis=1, keepdims=True)


def cut_rows(value, skip):
    return pltpu.roll(value, lax.rem(TALL - skip, TALL), 0)[:SIDE]


def add_window(acc, current, top, left):
    col = pl.multiple_of((left + LANES) // LANES * LANES, LANES)
    shift = left + LANES - col
    wide = jnp.concatenate([current, jnp.zeros_like(current)], axis=1)
    wide = pltpu.roll(wide, shift, 1)
    wide = jnp.concatenate([wide, jnp.zeros((8, WIDE), jnp.float32)], axis=0)
    wide = pltpu.roll(wide, lax.rem(top + RAD, 8), 0)
    rows = pl.ds(pl.multiple_of((top + RAD) // 8 * 8, 8), TALL)
    acc[rows, pl.ds(col, WIDE)] = acc[rows, pl.ds(col, WIDE)] + wide


def solver_parts(state):
    r_s, p_s, s_s, x_s, w_s, vd_s, vu_s, hr_s, hl_s, isd_s, inj_s, gnd_s, v_s, h_s = state
    row_id = lax.broadcasted_iota(jnp.int32, (SIDE, SIDE), 0)
    col_id = lax.broadcasted_iota(jnp.int32, (SIDE, SIDE), 1)

    def operate(b):
        here = r_s[b, 8:8 + SIDE, :]
        down = r_s[b, 9:9 + SIDE, :]
        up = r_s[b, 7:7 + SIDE, :]
        beside = vd_s[b] * down + vu_s[b] * up
        beside = beside + hr_s[b] * roll(here, -1, 1) + hl_s[b] * roll(here, 1, 1)
        applied = here - beside
        w_s[b] = applied
        return total(here * here), total(here * applied)

    def prepare(b, res, signed):
        res_down, res_right = roll(res, -1, 0), roll(res, -1, 1)
        has_down = (res > 0.0) & (res_down > 0.0) & (row_id < SIDE - 1)
        has_right = (res > 0.0) & (res_right > 0.0) & (col_id < SIDE - 1)
        vertical = jnp.where(has_down, 2.0 / jnp.where(has_down, res + res_down, 1.0), 0.0)
        horizontal = jnp.where(has_right, 2.0 / jnp.where(has_right, res + res_right, 1.0), 0.0)
        center = ((row_id == RAD) & (col_id == RAD)).astype(jnp.float32)
        inject = jnp.maximum(signed, 0.0) + center
        ground = jnp.maximum(-signed, 0.0)
        diagonal = vertical + roll(vertical, 1, 0) + horizontal + roll(horizontal, 1, 1) + ground + LEAKAGE
        isd = 1.0 / jnp.sqrt(diagonal)
        scaled_v = vertical * isd * roll(isd, -1, 0)
        scaled_h = horizontal * isd * roll(isd, -1, 1)
        v_s[b], h_s[b] = vertical, horizontal
        vd_s[b], vu_s[b] = scaled_v, roll(scaled_v, 1, 0)
        hr_s[b], hl_s[b] = scaled_h, roll(scaled_h, 1, 1)
        inj_s[b], gnd_s[b], isd_s[b] = inject, ground, isd
        r_s[b, 0:8, :] = jnp.zeros((8, SIDE), jnp.float32)
        r_s[b, 8 + SIDE:16 + SIDE, :] = jnp.zeros((8, SIDE), jnp.float32)
        r_s[b, 8:8 + SIDE, :] = inject * isd
        zero = jnp.zeros((SIDE, SIDE), jnp.float32)
        p_s[b], s_s[b], x_s[b] = zero, zero, zero

    def step(_, carry):
        after = []
        for b in range(GROUP):
            gamma, alpha, beta = carry[b]
            here = r_s[b, 8:8 + SIDE, :]
            direction = here + beta * p_s[b]
            applied = w_s[b] + beta * s_s[b]
            p_s[b] = direction
            s_s[b] = applied
            x_s[b] = x_s[b] + alpha * direction
            r_s[b, 8:8 + SIDE, :] = here - alpha * applied
        for b in range(GROUP):
            gamma, alpha, beta = carry[b]
            gamma_next, delta = operate(b)
            beta_next = gamma_next / gamma
            alpha_next = gamma_next / (delta - beta_next * gamma_next / alpha)
            after.append((gamma_next, alpha_next, beta_next))
        return tuple(after)

    def finish(b):
        isd, vertical, horizontal = isd_s[b], v_s[b], h_s[b]
        voltage = x_s[b] * isd
        flow_down = vertical * jnp.abs(voltage - roll(voltage, -1, 0))
        flow_right = horizontal * jnp.abs(voltage - roll(voltage, -1, 1))
        flow = flow_down + roll(flow_down, 1, 0) + flow_right + roll(flow_right, 1, 1)
        return 0.5 * (flow + inj_s[b] + gnd_s[b] * jnp.abs(voltage))

    def iterate():
        carry = []
        for b in range(GROUP):
            gamma, delta = operate(b)
            carry.append((gamma, gamma / delta, jnp.zeros_like(gamma)))
        lax.fori_loop(0, ITERS, step, tuple(carry))

    return prepare, iterate, finish


def spans_of(rows, cols):
    return {
        -1: (slice(0, RAD), slice(0, LANES)),
        0: (slice(RAD, RAD + rows), slice(LANES, LANES + cols)),
        1: (slice(RAD + rows, SIDE + rows), slice(LANES + cols, WIDE + cols)),
    }


def turn_own(res, source, target, skip, turn):
    source, target = source.astype(jnp.float32), target.astype(jnp.float32)
    mark = source - target * (1.0 - source)
    turn = lax.rem(WIDE + turn, WIDE)
    res = cut_rows(pltpu.roll(res, turn, 1)[:, :SIDE], skip)
    mark = cut_rows(pltpu.roll(mark, turn, 1)[:, :SIDE], skip)
    return res, mark


def cut_kernel(rows, cols, centers, live, *refs):
    raw, out, bufs, sems = refs[:3], refs[3], refs[4:7], refs[7]

    def place(slot):
        top, left = corner_of(centers, slot, rows, cols)
        return top, left, *clamped(top, left, rows, cols)

    def copies(slot):
        _, _, row, col = place(slot)
        return [
            pltpu.make_async_copy(src.at[pl.ds(row, TALL), pl.ds(col, WIDE)], dst.at[slot], sems.at[k, slot])
            for k, (src, dst) in enumerate(zip(raw, bufs))
        ]

    def begin(slot, _):
        for copy in copies(slot):
            copy.start()
        return 0

    def cut(slot, _):
        for copy in copies(slot):
            copy.wait()
        top, left, row, col = place(slot)
        res, mark = turn_own(*(buf[slot] for buf in bufs), top - row, col - left)
        out[0, slot] = res
        out[1, slot] = mark / res
        return 0

    lax.fori_loop(0, live[0], begin, 0)
    lax.fori_loop(0, live[0], cut, 0)


def inner_kernel(rows, cols, windows, *refs):
    raw = refs[:3]
    cur, outs = refs[3], dict(zip(SHIFTS, refs[4:12]))
    pieces, halos = dict(zip(SHIFTS, refs[12:20])), dict(zip(SHIFTS, refs[20:28]))
    frames = [refs[28 + 3 * k:31 + 3 * k] for k in range(4)]
    sems, send_sems, recv_sems = refs[40:43]
    prepare, iterate, finish = solver_parts(refs[43:])
    slots = windows.shape[1]
    found = neighbours()

    everything = pl.ds(0, rows)
    places = (
        (everything, pl.ds(0, LANES)),
        (everything, pl.ds(cols - LANES, LANES)),
        (pl.ds(0, RAD), pl.ds(0, cols)),
        (pl.ds(rows - RAD, RAD), pl.ds(0, cols)),
    )
    frame_copies = [
        [pltpu.make_async_copy(raw[k].at[places[f]], frames[f][k], sems.at[f, k]) for k in range(3)]
        for f in range(4)
    ]
    for copy in sum(frame_copies, []):
        copy.start()
    for at in SHIFTS:
        halos[at][...] = jnp.zeros_like(halos[at])
    greet(found)

    def strengths(frame, cut=slice(None)):
        res, source, target = (ref[cut] for ref in frame)
        source, target = source.astype(jnp.float32), target.astype(jnp.float32)
        conduct = 1.0 / res
        return res, source * conduct - target * (1.0 - source) * conduct

    for f, at in enumerate(((0, -1), (0, 1), (-1, 0), (1, 0))):
        for copy in frame_copies[f]:
            copy.wait()
        for k, value in enumerate(strengths(frames[f])):
            if at[1] == 0:
                pieces[at][k] = value
            else:
                squeeze = pack_low if at[1] < 0 else pack_high
                pieces[at][k] = squeeze(value)
                pieces[(-1, at[1])][k] = squeeze(value[:RAD])
                pieces[(1, at[1])][k] = squeeze(value[rows - RAD:])
    all_greeted(found)
    copies = transfers(found, pieces, halos, send_sems, recv_sems)
    start_all(copies)

    def solve_group(group, _):
        def ready(b, _):
            slot = group * GROUP + b
            prepare(b, windows[0, slot], windows[1, slot])
            return 0

        lax.fori_loop(0, GROUP, ready, 0)
        iterate()

        def done(b, _):
            cur[group * GROUP + b] = finish(b)
            return 0

        lax.fori_loop(0, GROUP, done, 0)
        return 0

    lax.fori_loop(0, slots // GROUP, solve_group, 0)
    finish_all(copies, landings(found, pieces, halos, send_sems, recv_sems))
    for at in SHIFTS:
        outs[at][...] = halos[at][...]


def return_kernel(*refs):
    pieces, outs, halos = (dict(zip(SHIFTS, refs[8 * k:8 * k + 8])) for k in range(3))
    send_sems, recv_sems = refs[24:]
    found = neighbours()
    for at in SHIFTS:
        halos[at][...] = jnp.zeros_like(halos[at])
    greet(found)
    all_greeted(found)
    copies = transfers(found, pieces, halos, send_sems, recv_sems)
    start_all(copies)
    finish_all(copies, landings(found, pieces, halos, send_sems, recv_sems))
    for at in SHIFTS:
        outs[at][...] = halos[at][...]


def border_kernel(rows, cols, centers, live, inner_cur, *refs):
    raw, halos = refs[:3], dict(zip(SHIFTS, refs[3:11]))
    out, outs = refs[11], dict(zip(SHIFTS, refs[12:20]))
    bufs, sems, order, ext, acc, out_sem = refs[20:23], *refs[23:28]
    prepare, iterate, finish = solver_parts(refs[28:])

    def copies(slot):
        top, left = corner_of(centers, slot, rows, cols)
        row, col = clamped(top, left, rows, cols)
        return [
            pltpu.make_async_copy(
                src.at[pl.ds(row, TALL), pl.ds(col, WIDE)],
                dst.at[slot, pl.ds(RAD, TALL), :],
                sems.at[k, slot],
            )
            for k, (src, dst) in enumerate(zip(raw, bufs))
        ]

    def classify(slot, count):
        top, left = corner_of(centers, slot, rows, cols)
        outer = jnp.logical_not(is_inner(top, left, rows, cols))

        @pl.when(outer)
        def _():
            order[count] = slot
            for copy in copies(slot):
                copy.start()

        return count + outer.astype(jnp.int32)

    count = lax.fori_loop(0, live[0], classify, jnp.int32(0))
    acc[...] = jnp.zeros_like(acc)
    spans = spans_of(rows, cols)
    for which in range(2):
        for dr in (-1, 1):
            ext[which, spans[dr][0], spans[0][1]] = halos[(dr, 0)][which]
        for dr in (-1, 0, 1):
            start, stop = spans[dr][0].start, spans[dr][0].stop
            middle = (start + stop) // 2
            for dc in (-1, 1):
                split = to_high if dc < 0 else to_low
                first, second = split(halos[(dr, dc)][which])
                ext[which, start:middle, spans[dc][1]] = first
                ext[which, middle:stop, spans[dc][1]] = second

    row_id = lax.broadcasted_iota(jnp.int32, (SIDE, SIDE), 0)
    col_id = lax.broadcasted_iota(jnp.int32, (SIDE, SIDE), 1)

    def fetch(slot):
        top, left = corner_of(centers, slot, rows, cols)
        row, col = clamped(top, left, rows, cols)
        take = pl.ds(pl.multiple_of((RAD + top - row) // 8 * 8, 8), TALL)
        res, source, target = (buf[slot, take, :] for buf in bufs)
        res, mark = turn_own(res, source, target, lax.rem(RAD + top - row, 8), col - left)
        at_row, at_col = row_id + top, col_id + left
        own = (at_row >= 0) & (at_row < rows) & (at_col >= 0) & (at_col < cols)
        base = pl.multiple_of((left + LANES) // LANES * LANES, LANES)
        back = lax.rem(WIDE + base - left - LANES, WIDE)
        span = pl.ds(pl.multiple_of((top + RAD) // 8 * 8, 8), TALL)
        outer = [
            cut_rows(pltpu.roll(ext[k, span, pl.ds(base, WIDE)], back, 1)[:, :SIDE], lax.rem(top + RAD, 8))
            for k in range(2)
        ]
        signed = jnp.where(own, mark / jnp.where(own, res, 1.0), outer[1])
        return jnp.where(own, res, outer[0]), signed

    def solve_group(group, _):
        def ready(b, _):
            at = group * GROUP + b
            slot = order[jnp.minimum(at, count - 1)]

            @pl.when(at < count)
            def _():
                for copy in copies(slot):
                    copy.wait()

            prepare(b, *fetch(slot))
            return 0

        lax.fori_loop(0, GROUP, ready, 0)
        iterate()

        def done(b, _):
            at = group * GROUP + b

            @pl.when(at < count)
            def _():
                top, left = corner_of(centers, order[at], rows, cols)
                add_window(acc, finish(b), top, left)

            return 0

        lax.fori_loop(0, GROUP, done, 0)
        return 0

    lax.fori_loop(0, (count + GROUP - 1) // GROUP, solve_group, 0)

    def place(slot, _):
        top, left = corner_of(centers, slot, rows, cols)

        @pl.when(is_inner(top, left, rows, cols))
        def _():
            add_window(acc, inner_cur[slot], top, left)

        return 0

    lax.fori_loop(0, live[0], place, 0)
    copy = pltpu.make_async_copy(acc.at[pl.ds(RAD, rows), pl.ds(LANES, cols)], out, out_sem)
    copy.start()
    for dr in (-1, 1):
        outs[(dr, 0)][...] = acc[spans[dr][0], spans[0][1]]
    for dr in (-1, 0, 1):
        for dc in (-1, 1):
            tile = acc[spans[dr][0], spans[dc][1]]
            outs[(dr, dc)][...] = pack_high(tile) if dc < 0 else pack_low(tile)
    copy.wait()


def fold_kernel(rows, cols, *refs):
    halos = dict(zip(SHIFTS, refs[1:9]))
    out, upper, lower, left, right, sems = refs[9:]
    last = cols - LANES
    inner_rows = rows - SIDE
    places = (
        (upper, pl.ds(0, RAD), pl.ds(0, cols)),
        (lower, pl.ds(rows - RAD, RAD), pl.ds(0, cols)),
        (left, pl.ds(RAD, inner_rows), pl.ds(0, LANES)),
        (right, pl.ds(RAD, inner_rows), pl.ds(last, LANES)),
    )
    fetch = [pltpu.make_async_copy(out.at[r, c], buf, sems.at[0, k]) for k, (buf, r, c) in enumerate(places)]
    store = [pltpu.make_async_copy(buf, out.at[r, c], sems.at[1, k]) for k, (buf, r, c) in enumerate(places)]
    for copy in fetch:
        copy.start()

    def spread(dr, dc):
        first, second = (to_low if dc < 0 else to_high)(halos[(dr, dc)][...])
        low = lane_ids(first.shape) < RAD
        keep = low if dc < 0 else jnp.logical_not(low)
        return jnp.where(keep, first, 0.0), jnp.where(keep, second, 0.0)

    for copy in fetch:
        copy.wait()
    half = rows // 2
    for dc, buf, at in ((-1, left, 0), (1, right, last)):
        first, second = spread(0, dc)
        buf[0:half - RAD] = buf[0:half - RAD] + first[RAD:]
        buf[half - RAD:inner_rows] = buf[half - RAD:inner_rows] + second[:half - RAD]
        upper[:, at:at + LANES] = upper[:, at:at + LANES] + first[:RAD]
        lower[:, at:at + LANES] = lower[:, at:at + LANES] + second[half - RAD:]
        for dr, strip in ((-1, upper), (1, lower)):
            one, two = spread(dr, dc)
            strip[:RAD // 2, at:at + LANES] = strip[:RAD // 2, at:at + LANES] + one
            strip[RAD // 2:, at:at + LANES] = strip[RAD // 2:, at:at + LANES] + two
    upper[...] = upper[...] + halos[(-1, 0)][...]
    lower[...] = lower[...] + halos[(1, 0)][...]
    for copy in store:
        copy.start()
    for copy in store:
        copy.wait()


def local(resistance, source_mask, target_mask, centers, live_counts):
    rows, cols = resistance.shape
    slots = centers.shape[0]
    f32, i32 = jnp.float32, jnp.int32
    smem = pl.BlockSpec(memory_space=pltpu.SMEM)
    vmem = pl.BlockSpec(memory_space=pltpu.VMEM)
    hbm = pl.BlockSpec(memory_space=pl.ANY)

    shapes = {
        at: (RAD if at[0] else rows, cols) if at[1] == 0 else ((RAD if at[0] else rows) // 2, LANES) for at in SHIFTS
    }
    pairs = [pltpu.VMEM((2, *shapes[at]), f32) for at in SHIFTS]
    strips = [pltpu.VMEM(shapes[at], f32) for at in SHIFTS]
    state = [pltpu.VMEM((GROUP, SIDE + 16, SIDE), f32)] + [pltpu.VMEM((GROUP, SIDE, SIDE), f32)] * 13
    kinds = (f32, i32, i32)
    frame_shapes = ((rows, LANES), (rows, LANES), (RAD, cols), (RAD, cols))

    windows = pl.pallas_call(
        functools.partial(cut_kernel, rows, cols),
        out_shape=jax.ShapeDtypeStruct((2, slots, SIDE, SIDE), f32),
        in_specs=[smem, smem, hbm, hbm, hbm],
        out_specs=vmem,
        scratch_shapes=[pltpu.VMEM((slots, TALL, WIDE), kind) for kind in kinds]
        + [pltpu.SemaphoreType.DMA((3, slots))],
        compiler_params=pltpu.CompilerParams(vmem_limit_bytes=16 << 20),
        name="cut",
    )(centers, live_counts, resistance, source_mask, target_mask)

    inner_cur, *halos = pl.pallas_call(
        functools.partial(inner_kernel, rows, cols),
        out_shape=[jax.ShapeDtypeStruct((slots, SIDE, SIDE), f32)]
        + [jax.ShapeDtypeStruct((2, *shapes[at]), f32) for at in SHIFTS],
        in_specs=[vmem, hbm, hbm, hbm],
        out_specs=[vmem] * 9,
        scratch_shapes=pairs
        + pairs
        + [pltpu.VMEM(shape, kind) for shape in frame_shapes for kind in kinds]
        + [pltpu.SemaphoreType.DMA((4, 3)), pltpu.SemaphoreType.DMA((8,)), pltpu.SemaphoreType.DMA((8,))]
        + state,
        compiler_params=pltpu.CompilerParams(vmem_limit_bytes=32 << 20, collective_id=0, has_side_effects=True),
        name="inner",
    )(windows, resistance, source_mask, target_mask)

    merged, *currents = pl.pallas_call(
        functools.partial(border_kernel, rows, cols),
        out_shape=[jax.ShapeDtypeStruct((rows, cols), f32)]
        + [jax.ShapeDtypeStruct(shapes[at], f32) for at in SHIFTS],
        in_specs=[smem, smem, vmem, hbm, hbm, hbm] + [vmem] * 8,
        out_specs=[hbm] + [vmem] * 8,
        scratch_shapes=[pltpu.VMEM((slots, TALL + SIDE, WIDE), kind) for kind in kinds]
        + [
            pltpu.SemaphoreType.DMA((3, slots)),
            pltpu.SMEM((slots,), i32),
            pltpu.VMEM((2, rows + SIDE, cols + WIDE), f32),
            pltpu.VMEM((rows + SIDE, cols + WIDE), f32),
            pltpu.SemaphoreType.DMA,
        ]
        + state,
        compiler_params=pltpu.CompilerParams(vmem_limit_bytes=45 << 20),
        name="border",
    )(centers, live_counts, inner_cur, resistance, source_mask, target_mask, *halos)

    back = pl.pallas_call(
        return_kernel,
        out_shape=[jax.ShapeDtypeStruct(shapes[at], f32) for at in SHIFTS],
        in_specs=[vmem] * 8,
        out_specs=[vmem] * 8,
        scratch_shapes=strips + [pltpu.SemaphoreType.DMA((8,)), pltpu.SemaphoreType.DMA((8,))],
        compiler_params=pltpu.CompilerParams(vmem_limit_bytes=8 << 20, collective_id=1, has_side_effects=True),
        name="give_back",
    )(*currents)
    out_shape = jax.ShapeDtypeStruct((rows, cols), f32)

    return pl.pallas_call(
        functools.partial(fold_kernel, rows, cols),
        out_shape=out_shape,
        in_specs=[hbm] + [vmem] * 8,
        out_specs=hbm,
        scratch_shapes=[
            pltpu.VMEM((RAD, cols), f32),
            pltpu.VMEM((RAD, cols), f32),
            pltpu.VMEM((rows - SIDE, LANES), f32),
            pltpu.VMEM((rows - SIDE, LANES), f32),
            pltpu.SemaphoreType.DMA((2, 4)),
        ],
        input_output_aliases={0: 0},
        compiler_params=pltpu.CompilerParams(vmem_limit_bytes=16 << 20),
        name="fold",
    )(merged, *back)


def solution(mesh):
    return jax.shard_map(
        local,
        mesh=mesh,
        in_specs=(
            P("row", "col"),
            P("row", "col"),
            P("row", "col"),
            P(("row", "col"), None),
            P(("row", "col")),
        ),
        out_specs=P("row", "col"),
        check_vma=False,
    )
```

profile of v0, /device:TPU:13, one launch (start us, length us, event | category | flops | bytes accessed | tf_op | source)
XLA Modules:
  0.0 100.7 jit_solution(13724415638377566953)
XLA Ops:
  0.7 0.8 copy.8.centers
  1.4 0.0 copy-start
  1.4 2.2 %copy-done = f32[1024,1024]{1,0:T(8,128)S(1)} copy-done((f32[1024,1024]{1,0:T(8,128)S(1)}, f32[1024,1024]{1,0:T(8,128)}, u32[]{:S(2)}) %copy-start) | copy-done | bytes 4194328
  3.6 0.0 copy-start.2
  3.6 2.2 %copy-done.2 = s32[1024,1024]{1,0:T(8,128)S(1)} copy-done((s32[1024,1024]{1,0:T(8,128)S(1)}, s32[1024,1024]{1,0:T(8,128)}, u32[]{:S(2)}) %copy-start.2) | copy-done | bytes 4194328
  5.8 0.0 copy-start.4
  5.8 2.2 %copy-done.4 = s32[1024,1024]{1,0:T(8,128)S(1)} copy-done((s32[1024,1024]{1,0:T(8,128)S(1)}, s32[1024,1024]{1,0:T(8,128)}, u32[]{:S(2)}) %copy-start.4) | copy-done | bytes 4194328
  8.0 0.0 copy-start.1
  8.0 0.0 copy-start.3
  8.0 0.0 copy-start.5
  8.0 1.6 %cut.1.windows = f32[2,16,128,128]{3,2,1,0:T(8,128)S(1)} custom-call(s32[16,2]{1,0:T(8,128)S(1)} %copy.8.centers, s32[1]{0:T(128)S(6)} %copy.10.live, f32[1024,1024]{1,0:T(8,128)S(1)} %copy-done, s32[1024,1024]{1,0:T(8,128)S(1)} %copy-done.2, s32[1024,1024]{1,0:T(8,128)S(1)} %copy-done.4), custom_call_target="tpu_custom_call" | custom-call | tf_op jit(solution)/shard_map/cut/pallas_call | solution.py:537
  9.6 0.5 copy-done.1
  10.2 1.3 %copy-done.3 = s32[1024,1024]{1,0:T(8,128)S(1)} copy-done((s32[1024,1024]{1,0:T(8,128)S(1)}, s32[1024,1024]{1,0:T(8,128)}, u32[]{:S(2)}) %copy-start.3) | copy-done | bytes 4194328
  11.4 1.2 %copy-done.5 = s32[1024,1024]{1,0:T(8,128)S(1)} copy-done((s32[1024,1024]{1,0:T(8,128)S(1)}, s32[1024,1024]{1,0:T(8,128)}, u32[]{:S(2)}) %copy-start.5) | copy-done | bytes 4194328
  12.6 46.4 %inner.1 = (f32[16,128,128]{2,1,0:T(8,128)S(1)}, f32[2,512,128]{2,1,0:T(8,128)S(1)}, f32[2,512,128]{2,1,0:T(8,128)S(1)}, f32[2,64,1024]{2,1,0:T(8,128)S(1)}, f32...) custom-call(f32[2,16,128,128]{3,2,1,0:T(8,128)S(1)} %cut.1.windows, ...), custom_call_target="tpu_custom_call" | custom-call | tf_op jit(solution)/shard_map/inner/pallas_call | solution.py:548
  59.1 4.2 %border.1 = (f32[1024,1024]{1,0:T(8,128)}, f32[512,128]{1,0:T(8,128)S(1)}, f32[512,128]{1,0:T(8,128)S(1)}, f32[64,1024]{1,0:T(8,128)S(1)}, f32[64,1024]{1,0:T(8,...) custom-call(s32[16,2]{1,0:T(8,128)S(1)} %copy.8.centers, ...), custom_call_target="tpu_custom_call" | custom-call | tf_op jit(solution)/shard_map/border/pallas_call | solution.py:563
  63.3 34.7 %give_back.1 = (f32[512,128]{1,0:T(8,128)S(1)}, f32[512,128]{1,0:T(8,128)S(1)}, f32[64,1024]{1,0:T(8,128)S(1)}, f32[64,1024]{1,0:T(8,128)S(1)}, f32[32,128]{1,0:...) custom-call(f32[512,128]{1,0:T(8,128)S(1)} %get-tuple-element.41.refs_0_, ...), custom_call_target="tpu_custom_call" | custom-call | tf_op jit(solution)/shard_map/give_back/pallas_call | solution.py:582
  98.0 2.7 %fold.1 = f32[1024,1024]{1,0:T(8,128)} custom-call(f32[1024,1024]{1,0:T(8,128)} %get-tuple-element.40.refs_0_, f32[512,128]{1,0:T(8,128)S(1)} %get-tuple-element.49.refs_1_, f32[512,128]{1,0:T(8,128)S(1)} %get-tuple-element.50.refs_2_, f32[64,1024]{1,0:T(8,128)S(1)} %get-tuple-element.51.refs_3_, ...), custom_call_target="tpu_custom_call", output_to_operand_aliasing={{}: (0, {})} | custom-call | tf_op jit(solution)/shard_map/fold/pallas_call | solution.py:593
Async XLA Ops:
  1.4 2.2 %copy-start = (f32[1024,1024]{1,0:T(8,128)S(1)}, f32[1024,1024]{1,0:T(8,128)}, u32[]{:S(2)}) copy-start(f32[1024,1024]{1,0:T(8,128)} %refs_0_.5) | copy-start | bytes 12582916
  3.6 2.2 %copy-start.2 = (s32[1024,1024]{1,0:T(8,128)S(1)}, s32[1024,1024]{1,0:T(8,128)}, u32[]{:S(2)}) copy-start(s32[1024,1024]{1,0:T(8,128)} %refs_1_.5) | copy-start | bytes 12582916
  5.8 2.2 %copy-start.4 = (s32[1024,1024]{1,0:T(8,128)S(1)}, s32[1024,1024]{1,0:T(8,128)}, u32[]{:S(2)}) copy-start(s32[1024,1024]{1,0:T(8,128)} %refs_2_.5) | copy-start | bytes 12582916
  8.0 2.2 %copy-start.1 = (f32[1024,1024]{1,0:T(8,128)S(1)}, f32[1024,1024]{1,0:T(8,128)}, u32[]{:S(2)}) copy-start(f32[1024,1024]{1,0:T(8,128)} %refs_0_.5) | copy-start | bytes 12582916
  8.0 3.5 %copy-start.3 = (s32[1024,1024]{1,0:T(8,128)S(1)}, s32[1024,1024]{1,0:T(8,128)}, u32[]{:S(2)}) copy-start(s32[1024,1024]{1,0:T(8,128)} %refs_1_.5) | copy-start | bytes 12582916
  8.0 4.7 %copy-start.5 = (s32[1024,1024]{1,0:T(8,128)S(1)}, s32[1024,1024]{1,0:T(8,128)}, u32[]{:S(2)}) copy-start(s32[1024,1024]{1,0:T(8,128)} %refs_2_.5) | copy-start | bytes 12582916
where the time goes:
time: 101 us
  Pallas kernels  89.7 us (89%)
  local copies, waits for them, and re-layouts  10.3 us (10%)
    pallas_call x1, Pallas kernels, local(): pl.pallas_call(functools.partial(inner_kernel, rows, cols), out_shape=[ja...  46.4 us
    pallas_call x1, Pallas kernels, local(): pl.pallas_call(return_kernel, out_shape=[jax.ShapeDtypeStruct(shapes[at],...  34.7 us
    unnamed x13, local copies, waits for them, and re-layouts  10.3 us
    pallas_call x1, Pallas kernels, local(): pl.pallas_call(functools.partial(border_kernel, rows, cols), out_shape=[j...  4.25 us
    pallas_call x1, Pallas kernels, local(): pl.pallas_call(functools.partial(fold_kernel, rows, cols), out_shape=out_...  2.68 us

commit v1 on v0

--- a/solution.py
+++ b/solution.py
@@ -11,7 +11,9 @@
 SIDE = 2 * RAD
 ITERS = 24
 LEAKAGE = 0.02
-GROUP = 4
+INNER_GROUP = 8
+BORDER_GROUP = 4
+CHUNK = 32
 LANES = 128
 TALL = SIDE + 8
 WIDE = 2 * LANES
@@ -147,20 +149,24 @@
     acc[rows, pl.ds(col, WIDE)] = acc[rows, pl.ds(col, WIDE)] + wide
 
 
-def solver_parts(state):
+def solver_parts(state, group_size):
     r_s, p_s, s_s, x_s, w_s, vd_s, vu_s, hr_s, hl_s, isd_s, inj_s, gnd_s, v_s, h_s = state
     row_id = lax.broadcasted_iota(jnp.int32, (SIDE, SIDE), 0)
     col_id = lax.broadcasted_iota(jnp.int32, (SIDE, SIDE), 1)
 
     def operate(b):
-        here = r_s[b, 8:8 + SIDE, :]
-        down = r_s[b, 9:9 + SIDE, :]
-        up = r_s[b, 7:7 + SIDE, :]
-        beside = vd_s[b] * down + vu_s[b] * up
-        beside = beside + hr_s[b] * roll(here, -1, 1) + hl_s[b] * roll(here, 1, 1)
-        applied = here - beside
-        w_s[b] = applied
-        return total(here * here), total(here * applied)
+        squares = jnp.zeros((8, SIDE), jnp.float32)
+        products = jnp.zeros((8, SIDE), jnp.float32)
+        for at in range(0, SIDE, CHUNK):
+            cut = slice(at, at + CHUNK)
+            here = r_s[b, at + 8:at + 8 + CHUNK, :]
+            beside = vd_s[b, cut] * r_s[b, at + 9:at + 9 + CHUNK, :] + vu_s[b, cut] * r_s[b, at + 7:at + 7 + CHUNK, :]
+            beside = beside + hr_s[b, cut] * roll(here, -1, 1) + hl_s[b, cut] * roll(here, 1, 1)
+            applied = here - beside
+            w_s[b, cut] = applied
+            squares = squares + jnp.sum((here * here).reshape(CHUNK // 8, 8, SIDE), axis=0)
+            products = products + jnp.sum((here * applied).reshape(CHUNK // 8, 8, SIDE), axis=0)
+        return total(squares), total(products)
 
     def prepare(b, res, signed):
         res_down, res_right = roll(res, -1, 0), roll(res, -1, 1)
@@ -187,21 +193,22 @@
 
     def step(_, carry):
         after = []
-        for b in range(GROUP):
-            gamma, alpha, beta = carry[b]
-            here = r_s[b, 8:8 + SIDE, :]
-            direction = here + beta * p_s[b]
-            applied = w_s[b] + beta * s_s[b]
-            p_s[b] = direction
-            s_s[b] = applied
-            x_s[b] = x_s[b] + alpha * direction
-            r_s[b, 8:8 + SIDE, :] = here - alpha * applied
-        for b in range(GROUP):
-            gamma, alpha, beta = carry[b]
-            gamma_next, delta = operate(b)
-            beta_next = gamma_next / gamma
-            alpha_next = gamma_next / (delta - beta_next * gamma_next / alpha)
-            after.append((gamma_next, alpha_next, beta_next))
+        for b in range(group_size):
+            alpha, beta, gamma_inv, alpha_inv = carry[b]
+            for at in range(0, SIDE, CHUNK):
+                cut, inset = slice(at, at + CHUNK), slice(at + 8, at + 8 + CHUNK)
+                here = r_s[b, inset]
+                direction = here + beta * p_s[b, cut]
+                applied = w_s[b, cut] + beta * s_s[b, cut]
+                p_s[b, cut] = direction
+                s_s[b, cut] = applied
+                x_s[b, cut] = x_s[b, cut] + alpha * direction
+                r_s[b, inset] = here - alpha * applied
+            gamma, delta = operate(b)
+            beta = gamma * gamma_inv
+            bottom = delta - beta * (gamma * alpha_inv)
+            gamma_inv = 1.0 / gamma
+            after.append((gamma / bottom, beta, gamma_inv, bottom * gamma_inv))
         return tuple(after)
 
     def finish(b):
@@ -214,10 +221,11 @@
 
     def iterate():
         carry = []
-        for b in range(GROUP):
+        for b in range(group_size):
             gamma, delta = operate(b)
-            carry.append((gamma, gamma / delta, jnp.zeros_like(gamma)))
-        lax.fori_loop(0, ITERS, step, tuple(carry))
+            gamma_inv = 1.0 / gamma
+            carry.append((gamma / delta, jnp.zeros_like(gamma), gamma_inv, delta * gamma_inv))
+        lax.fori_loop(0, ITERS, step, tuple(carry), unroll=2)
 
     return prepare, iterate, finish
 
@@ -277,7 +285,7 @@
     pieces, halos = dict(zip(SHIFTS, refs[12:20])), dict(zip(SHIFTS, refs[20:28]))
     frames = [refs[28 + 3 * k:31 + 3 * k] for k in range(4)]
     sems, send_sems, recv_sems = refs[40:43]
-    prepare, iterate, finish = solver_parts(refs[43:])
+    prepare, iterate, finish = solver_parts(refs[43:], INNER_GROUP)
     slots = windows.shape[1]
     found = neighbours()
 
@@ -321,21 +329,21 @@
 
     def solve_group(group, _):
         def ready(b, _):
-            slot = group * GROUP + b
+            slot = group * INNER_GROUP + b
             prepare(b, windows[0, slot], windows[1, slot])
             return 0
 
-        lax.fori_loop(0, GROUP, ready, 0)
+        lax.fori_loop(0, INNER_GROUP, ready, 0)
         iterate()
 
         def done(b, _):
-            cur[group * GROUP + b] = finish(b)
+            cur[group * INNER_GROUP + b] = finish(b)
             return 0
 
-        lax.fori_loop(0, GROUP, done, 0)
+        lax.fori_loop(0, INNER_GROUP, done, 0)
         return 0
 
-    lax.fori_loop(0, slots // GROUP, solve_group, 0)
+    lax.fori_loop(0, slots // INNER_GROUP, solve_group, 0)
     finish_all(copies, landings(found, pieces, halos, send_sems, recv_sems))
     for at in SHIFTS:
         outs[at][...] = halos[at][...]
@@ -360,7 +368,7 @@
     raw, halos = refs[:3], dict(zip(SHIFTS, refs[3:11]))
     out, outs = refs[11], dict(zip(SHIFTS, refs[12:20]))
     bufs, sems, order, ext, acc, out_sem = refs[20:23], *refs[23:28]
-    prepare, iterate, finish = solver_parts(refs[28:])
+    prepare, iterate, finish = solver_parts(refs[28:], BORDER_GROUP)
 
     def copies(slot):
         top, left = corner_of(centers, slot, rows, cols)
@@ -424,7 +432,7 @@
 
     def solve_group(group, _):
         def ready(b, _):
-            at = group * GROUP + b
+            at = group * BORDER_GROUP + b
             slot = order[jnp.minimum(at, count - 1)]
 
             @pl.when(at < count)
@@ -435,11 +443,11 @@
             prepare(b, *fetch(slot))
             return 0
 
-        lax.fori_loop(0, GROUP, ready, 0)
+        lax.fori_loop(0, BORDER_GROUP, ready, 0)
         iterate()
 
         def done(b, _):
-            at = group * GROUP + b
+            at = group * BORDER_GROUP + b
 
             @pl.when(at < count)
             def _():
@@ -448,10 +456,10 @@
 
             return 0
 
-        lax.fori_loop(0, GROUP, done, 0)
+        lax.fori_loop(0, BORDER_GROUP, done, 0)
         return 0
 
-    lax.fori_loop(0, (count + GROUP - 1) // GROUP, solve_group, 0)
+    lax.fori_loop(0, (count + BORDER_GROUP - 1) // BORDER_GROUP, solve_group, 0)
 
     def place(slot, _):
         top, left = corner_of(centers, slot, rows, cols)
@@ -523,14 +531,17 @@
     f32, i32 = jnp.float32, jnp.int32
     smem = pl.BlockSpec(memory_space=pltpu.SMEM)
     vmem = pl.BlockSpec(memory_space=pltpu.VMEM)
-    hbm = pl.BlockSpec(memory_space=pl.ANY)
+    hbm = pl.BlockSpec(memory_space=pltpu.HBM)
 
     shapes = {
         at: (RAD if at[0] else rows, cols) if at[1] == 0 else ((RAD if at[0] else rows) // 2, LANES) for at in SHIFTS
     }
     pairs = [pltpu.VMEM((2, *shapes[at]), f32) for at in SHIFTS]
     strips = [pltpu.VMEM(shapes[at], f32) for at in SHIFTS]
-    state = [pltpu.VMEM((GROUP, SIDE + 16, SIDE), f32)] + [pltpu.VMEM((GROUP, SIDE, SIDE), f32)] * 13
+
+    def state(group_size):
+        return [pltpu.VMEM((group_size, SIDE + 16, SIDE), f32)] + [pltpu.VMEM((group_size, SIDE, SIDE), f32)] * 13
+
     kinds = (f32, i32, i32)
     frame_shapes = ((rows, LANES), (rows, LANES), (RAD, cols), (RAD, cols))
 
@@ -541,7 +552,7 @@
         out_specs=vmem,
         scratch_shapes=[pltpu.VMEM((slots, TALL, WIDE), kind) for kind in kinds]
         + [pltpu.SemaphoreType.DMA((3, slots))],
-        compiler_params=pltpu.CompilerParams(vmem_limit_bytes=16 << 20),
+        compiler_params=pltpu.CompilerParams(vmem_limit_bytes=60 << 20),
         name="cut",
     )(centers, live_counts, resistance, source_mask, target_mask)
 
@@ -555,8 +566,8 @@
         + pairs
         + [pltpu.VMEM(shape, kind) for shape in frame_shapes for kind in kinds]
         + [pltpu.SemaphoreType.DMA((4, 3)), pltpu.SemaphoreType.DMA((8,)), pltpu.SemaphoreType.DMA((8,))]
-        + state,
-        compiler_params=pltpu.CompilerParams(vmem_limit_bytes=32 << 20, collective_id=0, has_side_effects=True),
+        + state(INNER_GROUP),
+        compiler_params=pltpu.CompilerParams(vmem_limit_bytes=60 << 20, collective_id=0, has_side_effects=True),
         name="inner",
     )(windows, resistance, source_mask, target_mask)
 
@@ -574,7 +585,7 @@
             pltpu.VMEM((rows + SIDE, cols + WIDE), f32),
             pltpu.SemaphoreType.DMA,
         ]
-        + state,
+        + state(BORDER_GROUP),
         compiler_params=pltpu.CompilerParams(vmem_limit_bytes=45 << 20),
         name="border",
     )(centers, live_counts, inner_cur, resistance, source_mask, target_mask, *halos)

time: 101 us -> 129 us (1.28)
  the two profiles are of different devices: /device:TPU:13 before, /device:TPU:11 now
where the time goes in v1:
time: 129 us
  Pallas kernels  116 us (90%)
  local copies, waits for them, and re-layouts  12 us (9%)
    pallas_call x1, Pallas kernels, local(): pl.pallas_call(functools.partial(inner_kernel, rows, cols), out_shape=[ja...  59 us
    pallas_call x1, Pallas kernels, local(): pl.pallas_call(functools.partial(border_kernel, rows, cols), out_shape=[j...  33.2 us
    pallas_call x1, Pallas kernels, local(): pl.pallas_call(return_kernel, out_shape=[jax.ShapeDtypeStruct(shapes[at],...  14.8 us
    unnamed x23, local copies, waits for them, and re-layouts  12 us
    pallas_call x1, Pallas kernels, local(): pl.pallas_call(functools.partial(cut_kernel, rows, cols), out_shape=jax.S...  6.39 us
    pallas_call x1, Pallas kernels, local(): pl.pallas_call(functools.partial(fold_kernel, rows, cols), out_shape=out_...  2.68 us

profile of v1, /device:TPU:11, one launch (start us, length us, event | category | flops | bytes accessed | tf_op | source)
XLA Modules:
  0.0 128.7 jit_solution(241607929485395919)
XLA Ops:
  0.7 1.3 %copy.8.centers = s32[16,2]{1,0:T(8,128)} copy(s32[16,2]{0,1:T(2,128)} %param.8) | data formatting | bytes 256 | tf_op args[3]
  2.0 6.4 %cut.1.windows = f32[2,16,128,128]{3,2,1,0:T(8,128)} custom-call(s32[16,2]{1,0:T(8,128)} %copy.8.centers, s32[1]{0:T(128)S(6)} %copy.10.live, f32[1024,1024]{1,0:T(8,128)} %refs_0_.5, s32[1024,1024]{1,0:T(8,128)} %refs_1_.5, s32[1024,1024]{1,0:T(8,128)} %refs_2_.5), custom_call_target="tpu_custom_call" | custom-call | tf_op jit(solution)/shard_map/cut/pallas_call | solution.py:548
  8.4 0.0 copy-start.6
  8.4 59.0 %inner.1 = (f32[16,128,128]{2,1,0:T(8,128)}, f32[2,512,128]{2,1,0:T(8,128)}, f32[2,512,128]{2,1,0:T(8,128)}, f32[2,64,1024]{2,1,0:T(8,128)}, f32[2,64,1024]{2,1,...) custom-call(f32[2,16,128,128]{3,2,1,0:T(8,128)} %cut.1.windows, ...), custom_call_target="tpu_custom_call" | custom-call | tf_op jit(solution)/shard_map/inner/pallas_call | solution.py:559
  67.5 0.0 copy-done.6
  67.5 0.0 copy-start
  67.5 2.2 %copy-done = f32[1024,1024]{1,0:T(8,128)S(1)} copy-done((f32[1024,1024]{1,0:T(8,128)S(1)}, f32[1024,1024]{1,0:T(8,128)}, u32[]{:S(2)}) %copy-start) | copy-done | bytes 4194328
  69.7 0.0 copy-start.1
  69.7 1.2 copy-done.1
  70.9 0.0 copy-start.2
  70.9 1.0 copy-done.2
  71.9 0.0 copy-start.3
  71.9 1.0 copy-done.3
  73.0 0.0 copy-start.4
  73.0 1.0 copy-done.4
  74.0 0.0 copy-start.5
  74.0 1.0 copy-done.5
  75.1 0.8 copy-done.7
  75.8 0.8 copy-done.8
  76.6 0.8 copy-done.9
  77.3 0.8 copy-done.10
  78.1 33.2 %border.1 = (f32[1024,1024]{1,0:T(8,128)}, f32[512,128]{1,0:T(8,128)S(1)}, f32[512,128]{1,0:T(8,128)S(1)}, f32[64,1024]{1,0:T(8,128)S(1)}, f32[64,1024]{1,0:T(8,...) custom-call(s32[16,2]{1,0:T(8,128)S(1)} %copy-done.6, ...), custom_call_target="tpu_custom_call" | custom-call | tf_op jit(solution)/shard_map/border/pallas_call | solution.py:574
  111.3 14.8 %give_back.1 = (f32[512,128]{1,0:T(8,128)S(1)}, f32[512,128]{1,0:T(8,128)S(1)}, f32[64,1024]{1,0:T(8,128)S(1)}, f32[64,1024]{1,0:T(8,128)S(1)}, f32[32,128]{1,0:...) custom-call(f32[512,128]{1,0:T(8,128)S(1)} %get-tuple-element.41.refs_0_, ...), custom_call_target="tpu_custom_call" | custom-call | tf_op jit(solution)/shard_map/give_back/pallas_call | solution.py:593
  126.0 2.7 %fold.1 = f32[1024,1024]{1,0:T(8,128)} custom-call(f32[1024,1024]{1,0:T(8,128)} %get-tuple-element.40.refs_0_, f32[512,128]{1,0:T(8,128)S(1)} %get-tuple-element.49.refs_1_, f32[512,128]{1,0:T(8,128)S(1)} %get-tuple-element.50.refs_2_, f32[64,1024]{1,0:T(8,128)S(1)} %get-tuple-element.51.refs_3_, ...), custom_call_target="tpu_custom_call", output_to_operand_aliasing={{}: (0, {})} | custom-call | tf_op jit(solution)/shard_map/fold/pallas_call | solution.py:604
  (4 shorter events, 0.0 us)
Async XLA Ops:
  8.4 59.1 %copy-start.6 = (s32[16,2]{1,0:T(8,128)S(1)}, s32[16,2]{1,0:T(8,128)}, u32[]{:S(2)}) copy-start(s32[16,2]{1,0:T(8,128)} %copy.8.centers) | copy-start | bytes 388
  67.5 2.2 %copy-start = (f32[1024,1024]{1,0:T(8,128)S(1)}, f32[1024,1024]{1,0:T(8,128)}, u32[]{:S(2)}) copy-start(f32[1024,1024]{1,0:T(8,128)} %refs_0_.5) | copy-start | bytes 12582916
  69.7 1.2 copy-start.1
  70.9 1.0 copy-start.2
  71.9 1.0 copy-start.3
  73.0 1.0 copy-start.4
  74.0 1.0 copy-start.5
  75.0 0.8 copy-start.7
  75.8 0.8 copy-start.8
  76.6 0.8 copy-start.9
  77.3 0.8 copy-start.10
